TPU v7x, 32 devices: a whole 2x2x4 slice. The times are simulated.
32 devices in a mesh: freq: 2 (over y), src: 8 (over z, x), rcv: 2 (over core).
Axes of the slice: x: 2, y: 2, z: 4, core: 2. Of those that a mesh axis runs over, the one named last changes fastest.
Arguments:
- panel: float32 [4, 1024, 5632], P('freq', 'src', 'rcv'), parts along dimension 0, may hold values from -6 to 6
- obliquity: float32 [4, 131072], P('freq'), parts along dimension 0, may hold values from -0.125 to 0.125
- panel_stations: int32 [1024], replicated, may hold values from 0 to 131071
- tile_map: int32 [512, 2], P('freq'), parts along dimension 0, may hold values from -1 to 21, as said below
- recorded: float32 [256, 4, 256, 256], P(('src', 'rcv'), 'freq'), parts along dimension 1, may hold values from -6 to 6
Outputs:
- demultiple: float32 [256, 4, 256, 256], P(('src', 'rcv'), 'freq'), parts along dimension 1
There are 2 independent parts, one for each index of `freq`. A program takes and returns all parts, laid end to end along the dimension named above; an argument that names none is the same for every part. Nothing has to cross between parts.
Inputs may be any that keep to these rules, and one draw needn't show every extreme that they name: `tile_map`: each slot holds a row tile i and a column tile j with j <= i; each of the 253 such tiles stands in exactly one slot; remaining slots hold -1 in both entries.
All inputs are finite; a program needn't handle non-finite values.
Results may differ from a plain program's by a relative error of at most 0.0044.
Values may be sent and summed in bfloat16 or wider, within the bound.
A program may use at most 192 MiB of HBM per device.

v0:
```python
import functools

import jax
import jax.numpy as jnp
from jax import lax
from jax.experimental import pallas as pl
from jax.experimental.pallas import tpu as pltpu
from jax.sharding import PartitionSpec as P

MESH = pl.DeviceIdType.MESH
pin = pltpu.with_memory_space_constraint
LANES = 128
ROWS = 8


def ring_position(index, n):
    if n % 2:
        return index
    half = index // 2
    odd = index % 2
    return odd * (n - 1 - half) + (1 - odd) * half


def ring_member(position, n):
    if n % 2:
        return position
    upper = position // (n // 2)
    return upper * (2 * (n - 1 - position) + 1) + (1 - upper) * 2 * position


def weighted_tile(weight, row_block, sign):
    spread = row_block.shape[-1] // LANES
    w_real = jnp.concatenate([weight[0] * sign] * spread, axis=1)
    w_imag = jnp.concatenate([weight[1] * sign] * spread, axis=1)
    p_real = row_block[0].astype(jnp.float32)
    p_imag = row_block[1].astype(jnp.float32)
    return [w_real * p_real - w_imag * p_imag, w_real * p_imag + w_imag * p_real]


def stack_rows(blocks):
    if blocks[0].shape[0] % 16:
        blocks = [b.astype(jnp.float32) for b in blocks]
    return jnp.concatenate(blocks, axis=0).astype(jnp.bfloat16)


def tile_product(weights, row_blocks, col_blocks, sign):
    lefts, reals, imags = [], [], []
    for weight, row_block, col_block in zip(weights, row_blocks, col_blocks):
        lefts += weighted_tile(weight, row_block, sign)
        reals += [col_block[0], -col_block[1]]
        imags += [col_block[1], col_block[0]]
    weighted = jnp.concatenate(lefts, axis=0).astype(jnp.bfloat16)
    form = (((0,), (0,)), ((), ()))
    return [
        lax.dot_general(weighted, stack_rows(c), form, preferred_element_type=jnp.float32)
        for c in (reals, imags)
    ]


def slot_tiles(tiles, at):
    row_tile, col_tile = tiles[0, at], tiles[1, at]
    sign = -(jnp.minimum(row_tile, 0) + 1).astype(jnp.float32)
    return jnp.maximum(row_tile, 0), jnp.maximum(col_tile, 0), sign


def pieces(held):
    size = -(-held // 4)
    return [(at, min(size, held - at)) for at in range(0, held, size)]


def gather_kernel(n_src, n_rcv, stations, tiles, panel, lines, recorded, acc, last, weight_out, *scratch):
    full = n_src // 2 - 1
    own = scratch[0]
    from_left = [own] + list(scratch[1 : 1 + full]) + [last]
    from_right = [own] + list(scratch[1 + full : 1 + 2 * full]) + [last]
    stage, obliquity, weight, ring_send, ring_recv, pair_send, pair_recv, last_sems, first_sems, load_sem, local_sem = scratch[1 + 2 * full :]

    src = lax.axis_index("src")
    rcv = lax.axis_index("rcv")
    kd, side = own.shape[2], own.shape[3]
    slots = acc.shape[0]
    held = own.shape[1] // n_rcv
    cuts = pieces(held)
    mine = pl.ds(rcv * held, held)
    pos = ring_position(src, n_src)
    right = ring_member((pos + 1) % n_src, n_src)
    left = ring_member((pos + n_src - 1) % n_src, n_src)

    barrier = pltpu.get_barrier_semaphore()
    for peer in (left, right):
        pl.semaphore_signal(barrier, inc=1, device_id={"src": peer}, device_id_type=MESH)
    for off in range(1, n_rcv):
        pl.semaphore_signal(barrier, inc=1, device_id={"rcv": (rcv + off) % n_rcv}, device_id_type=MESH)

    def load(part, c):
        at = (part, slice(None), pl.ds(cuts[c][0] * side, cuts[c][1] * side))
        return pltpu.make_async_copy(panel.at[at], stage.at[at], load_sem.at[part, c])

    for part in (0, 1):
        for c in range(len(cuts)):
            load(part, c).start()
    fetch = pltpu.make_async_copy(lines, obliquity, local_sem.at[0])
    fill = pltpu.make_async_copy(recorded, acc, local_sem.at[1])

    def convert(part, c):
        load(part, c).wait()
        for t in range(cuts[c][0], sum(cuts[c])):
            own[part, rcv * held + t] = stage[part, :, t * side : (t + 1) * side].astype(jnp.bfloat16)

    sides = ((0, from_left, right), (1, from_right, left))

    def ring_copy(d, step, part):
        _, blocks, peer = sides[d]
        return pltpu.make_async_remote_copy(
            src_ref=blocks[step].at[part, mine],
            dst_ref=blocks[step + 1].at[part, mine],
            send_sem=ring_send.at[d, step, part],
            recv_sem=ring_recv.at[d, step, part],
            device_id={"src": peer},
            device_id_type=MESH,
        )

    def pair_copy(d, step, part, off):
        block = sides[d][1][step].at[part, mine]
        return pltpu.make_async_remote_copy(
            src_ref=block,
            dst_ref=block,
            send_sem=pair_send.at[d, step, part, off - 1],
            recv_sem=pair_recv.at[d, step, part, off - 1],
            device_id={"rcv": (rcv + off) % n_rcv},
            device_id_type=MESH,
        )

    def first_ring(d, part, c):
        _, blocks, peer = sides[d]
        at = pl.ds(rcv * held + cuts[c][0], cuts[c][1])
        return pltpu.make_async_remote_copy(
            src_ref=own.at[part, at],
            dst_ref=blocks[1].at[part, at],
            send_sem=first_sems.at[0, d, part, c],
            recv_sem=first_sems.at[1, d, part, c],
            device_id={"src": peer},
            device_id_type=MESH,
        )

    def last_ring(d, c):
        _, blocks, peer = sides[d]
        at = pl.ds(rcv * held + cuts[c][0], cuts[c][1])
        return pltpu.make_async_remote_copy(
            src_ref=blocks[full].at[d, at],
            dst_ref=last.at[d, at],
            send_sem=last_sems.at[0, d, c, 0],
            recv_sem=last_sems.at[1, d, c, 0],
            device_id={"src": peer},
            device_id_type=MESH,
        )

    def last_pair(d, c, off):
        block = last.at[d, pl.ds(rcv * held + cuts[c][0], cuts[c][1])]
        return pltpu.make_async_remote_copy(
            src_ref=block,
            dst_ref=block,
            send_sem=last_sems.at[0, d, c, off],
            recv_sem=last_sems.at[1, d, c, off],
            device_id={"rcv": (rcv + off) % n_rcv},
            device_id_type=MESH,
        )

    def pairs(step, d):
        return d == 0 or step > 0

    def rows_of(owner):
        return pl.ds(pl.multiple_of(owner * kd, kd), kd)

    def product(blocks):
        def one(slot, carry):
            row_tile, col_tile, sign = slot_tiles(tiles, (src * n_rcv + rcv) * slots + slot)
            results = tile_product(
                [(weight[0, rows_of(owner), :], weight[1, rows_of(owner), :]) for _, owner in blocks],
                [jnp.stack([block[0, row_tile], block[1, row_tile]]) for block, _ in blocks],
                [(block[0, col_tile], block[1, col_tile]) for block, _ in blocks],
                sign,
            )
            for part in (0, 1):
                acc[slot, part] += results[part]
            return carry

        lax.fori_loop(0, slots, one, 0)

    def gather_weights():
        lane = lax.broadcasted_iota(jnp.int32, (ROWS, LANES), 1)
        row = lax.broadcasted_iota(jnp.int32, (ROWS, LANES), 0)

        def group(g, carry):
            real = jnp.zeros((ROWS, LANES), jnp.float32)
            imag = jnp.zeros((ROWS, LANES), jnp.float32)
            for u in range(ROWS):
                station = stations[g * ROWS + u]
                line = lax.div(station, LANES)
                pair = obliquity[line]
                hit = (row == u) & (lane == station - line * LANES)
                real = jnp.where(hit, pair[0:1], real)
                imag = jnp.where(hit, pair[1:2], imag)
            at = pl.ds(pl.multiple_of(g * ROWS, ROWS), ROWS)
            weight[0, at, :] = jnp.broadcast_to(jnp.sum(real, axis=1, keepdims=True), (ROWS, LANES))
            weight[1, at, :] = jnp.broadcast_to(jnp.sum(imag, axis=1, keepdims=True), (ROWS, LANES))
            return carry

        lax.fori_loop(0, weight.shape[1] // ROWS, group, 0)

    for part in (0, 1):
        for c in range(len(cuts)):
            convert(part, c)
            if part == 0 and c == 0:
                pl.semaphore_wait(barrier, 1 + n_rcv)
            for d in (0, 1):
                first_ring(d, part, c).start()
        for off in range(1, n_rcv):
            pair_copy(0, 0, part, off).start()
    for step in range(full + 1):
        for part in (0, 1):
            for d in (0, 1):
                if step == 0:
                    continue
                if step == 1:
                    for c in range(len(cuts)):
                        first_ring(d, part, c).wait_recv()
                else:
                    ring_copy(d, step - 1, part).wait_recv()
                if step < full:
                    ring_copy(d, step, part).start()
                elif part == d:
                    for c in range(len(cuts)):
                        last_ring(d, c).start()
                for off in range(1, n_rcv):
                    pair_copy(d, step, part, off).start()
        if step == 0:
            fetch.start()
            fill.start()
            fetch.wait()
            gather_weights()
            fill.wait()
        for part in (0, 1):
            for d in (0, 1):
                if pairs(step, d):
                    for off in range(1, n_rcv):
                        pair_copy(d, step, part, off).wait_recv()
        before = ring_member((pos + n_src - step) % n_src, n_src)
        after = ring_member((pos + step) % n_src, n_src)
        if step == 0:
            blocks = [(own, src)]
        else:
            blocks = [(from_left[step], before), (from_right[step], after)]
        product(blocks)

    opposite = ring_member((pos + n_src // 2) % n_src, n_src)
    weight_out[...] = weight[:, rows_of(opposite), :]
    for step in range(full + 1):
        for part in (0, 1):
            for d in (0, 1):
                if step == 0:
                    for c in range(len(cuts)):
                        first_ring(d, part, c).wait_send()
                elif step < full:
                    ring_copy(d, step, part).wait_send()
                if pairs(step, d):
                    for off in range(1, n_rcv):
                        pair_copy(d, step, part, off).wait_send()
    for c in range(len(cuts)):
        for d in (0, 1):
            last_ring(d, c).wait_recv()
            for off in range(1, n_rcv):
                last_pair(d, c, off).start()
    for c in range(len(cuts)):
        for d in (0, 1):
            for off in range(1, n_rcv):
                last_pair(d, c, off).wait_recv()
    for c in range(len(cuts)):
        for d in (0, 1):
            last_ring(d, c).wait_send()
            for off in range(1, n_rcv):
                last_pair(d, c, off).wait_send()


def finish_kernel(n_rcv, tiles, weight, last, acc, out, stage, out_sem):
    slots = acc.shape[0]
    device = lax.axis_index("src") * n_rcv + lax.axis_index("rcv")

    def put(slot):
        return pltpu.make_async_copy(stage.at[slot], out.at[slot], out_sem.at[slot])

    def one(slot, carry):
        row_tile, col_tile, sign = slot_tiles(tiles, device * slots + slot)
        results = tile_product(
            [(weight[0], weight[1])],
            [jnp.stack([last[0, row_tile], last[1, row_tile]])],
            [(last[0, col_tile], last[1, col_tile])],
            sign,
        )
        for part in (0, 1):
            stage[slot, part] = acc[slot, part] + results[part]
        put(slot).start()
        return carry

    def drain(slot, carry):
        put(slot).wait()
        return carry

    lax.fori_loop(0, slots, one, 0, unroll=2 if slots % 2 == 0 else 1)
    lax.fori_loop(0, slots, drain, 0)


def solution(mesh):
    n_src, n_rcv = mesh.shape["src"], mesh.shape["rcv"]
    assert n_src % 2 == 0 and n_src > 2

    def body(panel, obliquity, panel_stations, tile_map, recorded):
        kd, width = panel.shape[1], panel.shape[2]
        slots, _, side, _ = recorded.shape
        held = width // side
        full = n_src // 2 - 1
        lines = pin(obliquity.reshape(2, -1, LANES).transpose(1, 0, 2), pltpu.HBM)
        tiles = pin(tile_map.T, pltpu.HBM)
        stations = pin(panel_stations, pltpu.HBM)
        hbm = pl.BlockSpec(memory_space=pltpu.HBM)
        vmem = pl.BlockSpec(memory_space=pltpu.VMEM)
        smem = pl.BlockSpec(memory_space=pltpu.SMEM)
        dma = pltpu.SemaphoreType.DMA
        block = (2, n_rcv * held, kd, side)
        acc, last, weight = pl.pallas_call(
            functools.partial(gather_kernel, n_src, n_rcv),
            out_shape=(
                pltpu.VMEM(recorded.shape, recorded.dtype),
                pltpu.VMEM(block, jnp.bfloat16),
                pltpu.VMEM((2, kd, LANES), jnp.float32),
            ),
            in_specs=[smem, smem, hbm, hbm, hbm],
            out_specs=(vmem, vmem, vmem),
            scratch_shapes=[pltpu.VMEM(block, jnp.bfloat16)] * (1 + 2 * full)
            + [
                pltpu.VMEM(panel.shape, jnp.float32),
                pltpu.VMEM(lines.shape, jnp.float32),
                pltpu.VMEM((2, panel_stations.shape[0], LANES), jnp.float32),
                dma((2, full + 1, 2)),
                dma((2, full + 1, 2)),
                dma((2, full + 1, 2, n_rcv - 1)),
                dma((2, full + 1, 2, n_rcv - 1)),
                dma((2, 2, len(pieces(held)), n_rcv)),
                dma((2, 2, 2, len(pieces(held)))),
                dma((2, len(pieces(held)))),
                dma((2,)),
            ],
            compiler_params=pltpu.CompilerParams(
                collective_id=0, has_side_effects=True, vmem_limit_bytes=40 * 1024 * 1024
            ),
            name="ring_products",
        )(stations, tiles, pin(panel, pltpu.HBM), lines, pin(recorded, pltpu.HBM))
        return pl.pallas_call(
            functools.partial(finish_kernel, n_rcv),
            out_shape=jax.ShapeDtypeStruct(recorded.shape, recorded.dtype),
            in_specs=[smem, vmem, vmem, vmem],
            out_specs=hbm,
            scratch_shapes=[pltpu.VMEM(recorded.shape, recorded.dtype), dma((slots,))],
            compiler_params=pltpu.CompilerParams(vmem_limit_bytes=40 * 1024 * 1024),
            name="last_products",
        )(tiles, weight, last, acc)

    return jax.shard_map(
        body,
        mesh=mesh,
        in_specs=(
            P("freq", "src", "rcv"),
            P("freq", None),
            P(),
            P("freq", None),
            P(("src", "rcv"), "freq", None, None),
        ),
        out_specs=P(("src", "rcv"), "freq", None, None),
        check_vma=False,
    )
```

profile of v0, /device:TPU:0, one launch (start us, length us, event | category | flops | bytes accessed | tf_op | source)
XLA Modules:
  0.0 122.2 jit_solution(6803504146565736181)
XLA Ops:
  0.0 117.6 %ring_products.1 = (f32[16,2,256,256]{3,2,1,0:T(8,128)S(1)}, bf16[2,22,128,256]{3,2,1,0:T(8,128)(2,1)S(1)}, f32[2,128,128]{2,1,0:T(8,128)S(1)}) custom-call(s32[1024]{0:T(1024)} %stations.1, s32[2,256]{1,0:T(2,128)} %bitcast.5, f32[2,128,2816]{2,1,0:T(8,128)} %panel.1, f32[1024,2,128]{2,1,0:T(2,128)} %bitcast.4, f32[16,2,256,256]{3,2,1,0:T(8,128)} %recorded.1), custom_call_target="tpu_custom_call" | custom-call | tf_op jit(solution)/shard_map/ring_products/pallas_call | solution.py:330
  117.6 4.6 %last_products.1 = f32[16,2,256,256]{3,2,1,0:T(8,128)} custom-call(s32[2,256]{1,0:T(2,128)} %bitcast.6, f32[2,128,128]{2,1,0:T(8,128)S(1)} %get-tuple-element.8.weight, bf16[2,22,128,256]{3,2,1,0:T(8,128)(2,1)S(1)} %get-tuple-element.9.last, f32[16,2,256,256]{3,2,1,0:T(8,128)S(1)} %get-tuple-element.10.acc), custom_call_target="tpu_custom_call" | custom-call | tf_op jit(solution)/shard_map/last_products/pallas_call | solution.py:358
where the time goes:
time: 122 us
  Pallas kernels  122 us (100%)
    pallas_call x1, Pallas kernels, body(): pl.pallas_call(functools.partial(gather_kernel, n_src, n_rcv), out_shape=...  118 us
    pallas_call x1, Pallas kernels, body(): pl.pallas_call(functools.partial(finish_kernel, n_rcv), out_shape=jax.Sha...  4.56 us

commit v1 on v0

--- a/solution.py
+++ b/solution.py
@@ -64,16 +64,21 @@
 
 
 def pieces(held):
-    size = -(-held // 4)
-    return [(at, min(size, held - at)) for at in range(0, held, size)]
-
-
-def gather_kernel(n_src, n_rcv, stations, tiles, panel, lines, recorded, acc, last, weight_out, *scratch):
+    sizes = [1, 2]
+    while sum(sizes) < held - 3:
+        sizes.append(min(4, held - 3 - sum(sizes)))
+    sizes += [2, 1]
+    if sum(sizes) != held:
+        sizes = [1] * held
+    return [(sum(sizes[:i]), size) for i, size in enumerate(sizes)]
+
+
+def gather_kernel(n_src, n_rcv, stations_in, tiles_in, panel, lines, recorded, acc, last, weight_out, tiles, *scratch):
     full = n_src // 2 - 1
     own = scratch[0]
     from_left = [own] + list(scratch[1 : 1 + full]) + [last]
     from_right = [own] + list(scratch[1 + full : 1 + 2 * full]) + [last]
-    stage, obliquity, weight, ring_send, ring_recv, pair_send, pair_recv, last_sems, first_sems, load_sem, local_sem = scratch[1 + 2 * full :]
+    stage, obliquity, weight, stations, ring_send, ring_recv, pair_send, pair_recv, last_sems, first_sems, load_sem, local_sem = scratch[1 + 2 * full :]
 
     src = lax.axis_index("src")
     rcv = lax.axis_index("rcv")
@@ -86,19 +91,23 @@
     right = ring_member((pos + 1) % n_src, n_src)
     left = ring_member((pos + n_src - 1) % n_src, n_src)
 
+    def load(part, c):
+        at = (part, slice(None), pl.ds(cuts[c][0] * side, cuts[c][1] * side))
+        return pltpu.make_async_copy(panel.at[at], stage.at[at], load_sem.at[part, c])
+
+    for part in (0, 1):
+        load(part, 0).start()
     barrier = pltpu.get_barrier_semaphore()
     for peer in (left, right):
         pl.semaphore_signal(barrier, inc=1, device_id={"src": peer}, device_id_type=MESH)
     for off in range(1, n_rcv):
         pl.semaphore_signal(barrier, inc=1, device_id={"rcv": (rcv + off) % n_rcv}, device_id_type=MESH)
 
-    def load(part, c):
-        at = (part, slice(None), pl.ds(cuts[c][0] * side, cuts[c][1] * side))
-        return pltpu.make_async_copy(panel.at[at], stage.at[at], load_sem.at[part, c])
-
-    for part in (0, 1):
-        for c in range(len(cuts)):
+    for c in range(1, len(cuts)):
+        for part in (0, 1):
             load(part, c).start()
+    named = pltpu.make_async_copy(stations_in, stations, local_sem.at[2])
+    mapped = pltpu.make_async_copy(tiles_in, tiles, local_sem.at[3])
     fetch = pltpu.make_async_copy(lines, obliquity, local_sem.at[0])
     fill = pltpu.make_async_copy(recorded, acc, local_sem.at[1])
 
@@ -208,18 +217,22 @@
 
         lax.fori_loop(0, weight.shape[1] // ROWS, group, 0)
 
-    for part in (0, 1):
-        for c in range(len(cuts)):
+    for c in range(len(cuts)):
+        for part in (0, 1):
             convert(part, c)
             if part == 0 and c == 0:
                 pl.semaphore_wait(barrier, 1 + n_rcv)
-            for d in (0, 1):
-                first_ring(d, part, c).start()
+            first_ring(part, part, c).start()
+    for d in (0, 1):
+        for c in range(len(cuts)):
+            first_ring(d, 1 - d, c).start()
+    for part in (0, 1):
         for off in range(1, n_rcv):
             pair_copy(0, 0, part, off).start()
     for step in range(full + 1):
-        for part in (0, 1):
+        for turn in (0, 1):
             for d in (0, 1):
+                part = d if turn == 0 else 1 - d
                 if step == 0:
                     continue
                 if step == 1:
@@ -236,8 +249,12 @@
                     pair_copy(d, step, part, off).start()
         if step == 0:
             fetch.start()
+            named.start()
+            mapped.start()
             fill.start()
             fetch.wait()
+            named.wait()
+            mapped.wait()
             gather_weights()
             fill.wait()
         for part in (0, 1):
@@ -327,20 +344,22 @@
         smem = pl.BlockSpec(memory_space=pltpu.SMEM)
         dma = pltpu.SemaphoreType.DMA
         block = (2, n_rcv * held, kd, side)
-        acc, last, weight = pl.pallas_call(
+        acc, last, weight, mapped = pl.pallas_call(
             functools.partial(gather_kernel, n_src, n_rcv),
             out_shape=(
                 pltpu.VMEM(recorded.shape, recorded.dtype),
                 pltpu.VMEM(block, jnp.bfloat16),
                 pltpu.VMEM((2, kd, LANES), jnp.float32),
+                pltpu.SMEM(tiles.shape, tiles.dtype),
             ),
-            in_specs=[smem, smem, hbm, hbm, hbm],
-            out_specs=(vmem, vmem, vmem),
+            in_specs=[hbm] * 5,
+            out_specs=(vmem, vmem, vmem, smem),
             scratch_shapes=[pltpu.VMEM(block, jnp.bfloat16)] * (1 + 2 * full)
             + [
                 pltpu.VMEM(panel.shape, jnp.float32),
                 pltpu.VMEM(lines.shape, jnp.float32),
                 pltpu.VMEM((2, panel_stations.shape[0], LANES), jnp.float32),
+                pltpu.SMEM(panel_stations.shape, panel_stations.dtype),
                 dma((2, full + 1, 2)),
                 dma((2, full + 1, 2)),
                 dma((2, full + 1, 2, n_rcv - 1)),
@@ -348,7 +367,7 @@
                 dma((2, 2, len(pieces(held)), n_rcv)),
                 dma((2, 2, 2, len(pieces(held)))),
                 dma((2, len(pieces(held)))),
-                dma((2,)),
+                dma((4,)),
             ],
             compiler_params=pltpu.CompilerParams(
                 collective_id=0, has_side_effects=True, vmem_limit_bytes=40 * 1024 * 1024
@@ -363,7 +382,7 @@
             scratch_shapes=[pltpu.VMEM(recorded.shape, recorded.dtype), dma((slots,))],
             compiler_params=pltpu.CompilerParams(vmem_limit_bytes=40 * 1024 * 1024),
             name="last_products",
-        )(tiles, weight, last, acc)
+        )(mapped, weight, last, acc)
 
     return jax.shard_map(
         body,

time: 122 us -> 120 us (0.984)
  Pallas kernels: 122 us -> 120 us
    pallas_call x1, Pallas kernels: 118 us -> 116 us  [body(): pl.pallas_call(functools.partial(gather_kernel, n_src, n_rcv), out_shape=...]
where the time goes in v1:
time: 120 us
  Pallas kernels  120 us (100%)
    pallas_call x1, Pallas kernels, body(): pl.pallas_call(functools.partial(gather_kernel, n_src, n_rcv), out_shape=...  116 us
    pallas_call x1, Pallas kernels, body(): pl.pallas_call(functools.partial(finish_kernel, n_rcv), out_shape=jax.Sha...  3.87 us

profile of v1, /device:TPU:0, one launch (start us, length us, event | category | flops | bytes accessed | tf_op | source)
XLA Modules:
  0.0 119.5 jit_solution(976403973268652460)
XLA Ops:
  0.0 115.7 %ring_products.1 = (f32[16,2,256,256]{3,2,1,0:T(8,128)S(1)}, bf16[2,22,128,256]{3,2,1,0:T(8,128)(2,1)S(1)}, f32[2,128,128]{2,1,0:T(8,128)S(1)}, s32[2,256]{1,0:T(2,128)S(4)}) custom-call(s32[1024]{0:T(1024)} %stations_in.1, s32[2,256]{1,0:T(2,128)} %bitcast.5, f32[2,128,2816]{2,1,0:T(8,128)} %panel.1, f32[1024,2,128]{2,1,0:T(2,128)} %bitcast.4, ...), custom_call_target="tpu_custom_call" | custom-call | tf_op jit(solution)/shard_map/ring_products/pallas_call | solution.py:347
  115.7 3.9 %last_products.1 = f32[16,2,256,256]{3,2,1,0:T(8,128)} custom-call(s32[2,256]{1,0:T(2,128)S(4)} %get-tuple-element.9.tiles, f32[2,128,128]{2,1,0:T(8,128)S(1)} %get-tuple-element.10.weight, bf16[2,22,128,256]{3,2,1,0:T(8,128)(2,1)S(1)} %get-tuple-element.11.last, f32[16,2,256,256]{3,2,1,0:T(8,128)S(1)} %get-tuple-element.12.acc), custom_call_target="tpu_custom_call" | custom-call | tf_op jit(solution)/shard_map/last_products/pallas_call | solution.py:377

commit v2 on v1

--- a/solution.py
+++ b/solution.py
@@ -63,14 +63,12 @@
     return jnp.maximum(row_tile, 0), jnp.maximum(col_tile, 0), sign
 
 
-def pieces(held):
-    sizes = [1, 2]
-    while sum(sizes) < held - 3:
-        sizes.append(min(4, held - 3 - sum(sizes)))
-    sizes += [2, 1]
-    if sum(sizes) != held:
-        sizes = [1] * held
-    return [(sum(sizes[:i]), size) for i, size in enumerate(sizes)]
+def pieces(held, small_first):
+    small = min(2, held - 1) if small_first else 1
+    if small_first:
+        return [(0, small), (small, held - small)]
+    half = (held - small) * 2 // 3
+    return [(0, half), (half, held - small - half), (held - small, small)]
 
 
 def gather_kernel(n_src, n_rcv, stations_in, tiles_in, panel, lines, recorded, acc, last, weight_out, tiles, *scratch):
@@ -85,7 +83,8 @@
     kd, side = own.shape[2], own.shape[3]
     slots = acc.shape[0]
     held = own.shape[1] // n_rcv
-    cuts = pieces(held)
+    cuts = pieces(held, True)
+    ends = pieces(held, False)
     mine = pl.ds(rcv * held, held)
     pos = ring_position(src, n_src)
     right = ring_member((pos + 1) % n_src, n_src)
@@ -140,21 +139,21 @@
             device_id_type=MESH,
         )
 
-    def first_ring(d, part, c):
+    def first_ring(d, c):
         _, blocks, peer = sides[d]
         at = pl.ds(rcv * held + cuts[c][0], cuts[c][1])
         return pltpu.make_async_remote_copy(
-            src_ref=own.at[part, at],
-            dst_ref=blocks[1].at[part, at],
-            send_sem=first_sems.at[0, d, part, c],
-            recv_sem=first_sems.at[1, d, part, c],
+            src_ref=own.at[d, at],
+            dst_ref=blocks[1].at[d, at],
+            send_sem=first_sems.at[0, d, c],
+            recv_sem=first_sems.at[1, d, c],
             device_id={"src": peer},
             device_id_type=MESH,
         )
 
     def last_ring(d, c):
         _, blocks, peer = sides[d]
-        at = pl.ds(rcv * held + cuts[c][0], cuts[c][1])
+        at = pl.ds(rcv * held + ends[c][0], ends[c][1])
         return pltpu.make_async_remote_copy(
             src_ref=blocks[full].at[d, at],
             dst_ref=last.at[d, at],
@@ -165,7 +164,7 @@
         )
 
     def last_pair(d, c, off):
-        block = last.at[d, pl.ds(rcv * held + cuts[c][0], cuts[c][1])]
+        block = last.at[d, pl.ds(rcv * held + ends[c][0], ends[c][1])]
         return pltpu.make_async_remote_copy(
             src_ref=block,
             dst_ref=block,
@@ -222,10 +221,9 @@
             convert(part, c)
             if part == 0 and c == 0:
                 pl.semaphore_wait(barrier, 1 + n_rcv)
-            first_ring(part, part, c).start()
+            first_ring(part, c).start()
     for d in (0, 1):
-        for c in range(len(cuts)):
-            first_ring(d, 1 - d, c).start()
+        ring_copy(d, 0, 1 - d).start()
     for part in (0, 1):
         for off in range(1, n_rcv):
             pair_copy(0, 0, part, off).start()
@@ -235,15 +233,15 @@
                 part = d if turn == 0 else 1 - d
                 if step == 0:
                     continue
-                if step == 1:
+                if step == 1 and part == d:
                     for c in range(len(cuts)):
-                        first_ring(d, part, c).wait_recv()
+                        first_ring(d, c).wait_recv()
                 else:
                     ring_copy(d, step - 1, part).wait_recv()
                 if step < full:
                     ring_copy(d, step, part).start()
                 elif part == d:
-                    for c in range(len(cuts)):
+                    for c in range(len(ends)):
                         last_ring(d, c).start()
                 for off in range(1, n_rcv):
                     pair_copy(d, step, part, off).start()
@@ -275,24 +273,24 @@
     for step in range(full + 1):
         for part in (0, 1):
             for d in (0, 1):
-                if step == 0:
+                if step == 0 and part == d:
                     for c in range(len(cuts)):
-                        first_ring(d, part, c).wait_send()
+                        first_ring(d, c).wait_send()
                 elif step < full:
                     ring_copy(d, step, part).wait_send()
                 if pairs(step, d):
                     for off in range(1, n_rcv):
                         pair_copy(d, step, part, off).wait_send()
-    for c in range(len(cuts)):
+    for c in range(len(ends)):
         for d in (0, 1):
             last_ring(d, c).wait_recv()
             for off in range(1, n_rcv):
                 last_pair(d, c, off).start()
-    for c in range(len(cuts)):
+    for c in range(len(ends)):
         for d in (0, 1):
             for off in range(1, n_rcv):
                 last_pair(d, c, off).wait_recv()
-    for c in range(len(cuts)):
+    for c in range(len(ends)):
         for d in (0, 1):
             last_ring(d, c).wait_send()
             for off in range(1, n_rcv):
@@ -323,7 +321,7 @@
         put(slot).wait()
         return carry
 
-    lax.fori_loop(0, slots, one, 0, unroll=2 if slots % 2 == 0 else 1)
+    lax.fori_loop(0, slots, one, 0, unroll=4 if slots % 4 == 0 else 1)
     lax.fori_loop(0, slots, drain, 0)
 
 
@@ -364,9 +362,9 @@
                 dma((2, full + 1, 2)),
                 dma((2, full + 1, 2, n_rcv - 1)),
                 dma((2, full + 1, 2, n_rcv - 1)),
-                dma((2, 2, len(pieces(held)), n_rcv)),
-                dma((2, 2, 2, len(pieces(held)))),
-                dma((2, len(pieces(held)))),
+                dma((2, 2, len(pieces(held, False)), n_rcv)),
+                dma((2, 2, len(pieces(held, True)))),
+                dma((2, len(pieces(held, True)))),
                 dma((4,)),
             ],
             compiler_params=pltpu.CompilerParams(

time: 120 us -> 119 us (level)
  no operation moved by 1% of the time
where the time goes in v2:
time: 119 us
  Pallas kernels  119 us (100%)
    pallas_call x1, Pallas kernels, body(): pl.pallas_call(functools.partial(gather_kernel, n_src, n_rcv), out_shape=...  115 us
    pallas_call x1, Pallas kernels, body(): pl.pallas_call(functools.partial(finish_kernel, n_rcv), out_shape=jax.Sha...  3.72 us

profile of v2, /device:TPU:0, one launch (start us, length us, event | category | flops | bytes accessed | tf_op | source)
XLA Modules:
  0.0 118.8 jit_solution(10440287766785261284)
XLA Ops:
  0.0 115.0 %ring_products.1 = (f32[16,2,256,256]{3,2,1,0:T(8,128)S(1)}, bf16[2,22,128,256]{3,2,1,0:T(8,128)(2,1)S(1)}, f32[2,128,128]{2,1,0:T(8,128)S(1)}, s32[2,256]{1,0:T(2,128)S(4)}) custom-call(s32[1024]{0:T(1024)} %stations_in.1, s32[2,256]{1,0:T(2,128)} %bitcast.5, f32[2,128,2816]{2,1,0:T(8,128)} %panel.1, f32[1024,2,128]{2,1,0:T(2,128)} %bitcast.4, ...), custom_call_target="tpu_custom_call" | custom-call | tf_op jit(solution)/shard_map/ring_products/pallas_call | solution.py:345
  115.0 3.7 %last_products.1 = f32[16,2,256,256]{3,2,1,0:T(8,128)} custom-call(s32[2,256]{1,0:T(2,128)S(4)} %get-tuple-element.9.tiles, f32[2,128,128]{2,1,0:T(8,128)S(1)} %get-tuple-element.10.weight, bf16[2,22,128,256]{3,2,1,0:T(8,128)(2,1)S(1)} %get-tuple-element.11.last, f32[16,2,256,256]{3,2,1,0:T(8,128)S(1)} %get-tuple-element.12.acc), custom_call_target="tpu_custom_call" | custom-call | tf_op jit(solution)/shard_map/last_products/pallas_call | solution.py:375

commit v3 on v2

--- a/solution.py
+++ b/solution.py
@@ -63,12 +63,15 @@
     return jnp.maximum(row_tile, 0), jnp.maximum(col_tile, 0), sign
 
 
-def pieces(held, small_first):
-    small = min(2, held - 1) if small_first else 1
-    if small_first:
-        return [(0, small), (small, held - small)]
-    half = (held - small) * 2 // 3
-    return [(0, half), (half, held - small - half), (held - small, small)]
+def first_pieces(held):
+    small = min(2, held - 1)
+    return [(0, small), (small, held - small)]
+
+
+def last_pieces(n_rcv, held):
+    if n_rcv != 2 or held < 6:
+        return [[(r * held, held - 1), (r * held + held - 1, 1)] for r in range(n_rcv)]
+    return [[(0, held - 3), (held - 3, 2)], [(held + 1, held - 1), (held - 1, 2)]]
 
 
 def gather_kernel(n_src, n_rcv, stations_in, tiles_in, panel, lines, recorded, acc, last, weight_out, tiles, *scratch):
@@ -76,15 +79,15 @@
     own = scratch[0]
     from_left = [own] + list(scratch[1 : 1 + full]) + [last]
     from_right = [own] + list(scratch[1 + full : 1 + 2 * full]) + [last]
-    stage, obliquity, weight, stations, ring_send, ring_recv, pair_send, pair_recv, last_sems, first_sems, load_sem, local_sem = scratch[1 + 2 * full :]
+    stage, obliquity, weight, stations, ring_send, ring_recv, pair_send, pair_recv, last_sems, spread_sems, first_sems, load_sem, local_sem = scratch[1 + 2 * full :]
 
     src = lax.axis_index("src")
     rcv = lax.axis_index("rcv")
     kd, side = own.shape[2], own.shape[3]
     slots = acc.shape[0]
     held = own.shape[1] // n_rcv
-    cuts = pieces(held, True)
-    ends = pieces(held, False)
+    cuts = first_pieces(held)
+    plans = last_pieces(n_rcv, held)
     mine = pl.ds(rcv * held, held)
     pos = ring_position(src, n_src)
     right = ring_member((pos + 1) % n_src, n_src)
@@ -151,28 +154,49 @@
             device_id_type=MESH,
         )
 
-    def last_ring(d, c):
+    def last_ring(core, d, c):
         _, blocks, peer = sides[d]
-        at = pl.ds(rcv * held + ends[c][0], ends[c][1])
+        at = (d, pl.ds(*plans[core][c]))
         return pltpu.make_async_remote_copy(
-            src_ref=blocks[full].at[d, at],
-            dst_ref=last.at[d, at],
-            send_sem=last_sems.at[0, d, c, 0],
-            recv_sem=last_sems.at[1, d, c, 0],
+            src_ref=blocks[full].at[at],
+            dst_ref=last.at[at],
+            send_sem=last_sems.at[0, d, c],
+            recv_sem=last_sems.at[1, d, c],
             device_id={"src": peer},
             device_id_type=MESH,
         )
 
-    def last_pair(d, c, off):
-        block = last.at[d, pl.ds(rcv * held + ends[c][0], ends[c][1])]
+    def last_pair(core, c, off):
+        block = last.at[:, pl.ds(*plans[core][c])]
         return pltpu.make_async_remote_copy(
             src_ref=block,
             dst_ref=block,
-            send_sem=last_sems.at[0, d, c, off],
-            recv_sem=last_sems.at[1, d, c, off],
+            send_sem=spread_sems.at[0, c, off],
+            recv_sem=spread_sems.at[1, c, off],
             device_id={"rcv": (rcv + off) % n_rcv},
             device_id_type=MESH,
         )
+
+    def start_last(d, c):
+        for core in range(n_rcv):
+            pl.when(rcv == core)(lambda core=core: last_ring(core, d, c).start())
+
+    def finish_last(core):
+        others = [other for other in range(n_rcv) if other != core]
+        for c in (0, 1):
+            for d in (0, 1):
+                last_ring(core, d, c).wait_recv()
+            for off in range(1, n_rcv):
+                last_pair(core, c, off).start()
+        for c in (0, 1):
+            for d in (0, 1):
+                last_ring(core, d, c).wait_send()
+        for c in (0, 1):
+            for other in others:
+                last_pair(other, c, (core - other) % n_rcv).wait_recv()
+            for off in range(1, n_rcv):
+                last_pair(core, c, off).wait_send()
+
 
     def pairs(step, d):
         return d == 0 or step > 0
@@ -241,8 +265,7 @@
                 if step < full:
                     ring_copy(d, step, part).start()
                 elif part == d:
-                    for c in range(len(ends)):
-                        last_ring(d, c).start()
+                    start_last(d, 0)
                 for off in range(1, n_rcv):
                     pair_copy(d, step, part, off).start()
         if step == 0:
@@ -260,6 +283,9 @@
                 if pairs(step, d):
                     for off in range(1, n_rcv):
                         pair_copy(d, step, part, off).wait_recv()
+        if step == full:
+            for d in (0, 1):
+                start_last(d, 1)
         before = ring_member((pos + n_src - step) % n_src, n_src)
         after = ring_member((pos + step) % n_src, n_src)
         if step == 0:
@@ -281,20 +307,8 @@
                 if pairs(step, d):
                     for off in range(1, n_rcv):
                         pair_copy(d, step, part, off).wait_send()
-    for c in range(len(ends)):
-        for d in (0, 1):
-            last_ring(d, c).wait_recv()
-            for off in range(1, n_rcv):
-                last_pair(d, c, off).start()
-    for c in range(len(ends)):
-        for d in (0, 1):
-            for off in range(1, n_rcv):
-                last_pair(d, c, off).wait_recv()
-    for c in range(len(ends)):
-        for d in (0, 1):
-            last_ring(d, c).wait_send()
-            for off in range(1, n_rcv):
-                last_pair(d, c, off).wait_send()
+    for core in range(n_rcv):
+        pl.when(rcv == core)(functools.partial(finish_last, core))
 
 
 def finish_kernel(n_rcv, tiles, weight, last, acc, out, stage, out_sem):
@@ -362,9 +376,10 @@
                 dma((2, full + 1, 2)),
                 dma((2, full + 1, 2, n_rcv - 1)),
                 dma((2, full + 1, 2, n_rcv - 1)),
-                dma((2, 2, len(pieces(held, False)), n_rcv)),
-                dma((2, 2, len(pieces(held, True)))),
-                dma((2, len(pieces(held, True)))),
+                dma((2, 2, 2)),
+                dma((2, 2, n_rcv)),
+                dma((2, 2, len(first_pieces(held)))),
+                dma((2, len(first_pieces(held)))),
                 dma((4,)),
             ],
             compiler_params=pltpu.CompilerParams(

time: 119 us -> 119 us (level)
  no operation moved by 1% of the time
where the time goes in v3:
time: 119 us
  Pallas kernels  119 us (100%)
    pallas_call x1, Pallas kernels, body(): pl.pallas_call(functools.partial(gather_kernel, n_src, n_rcv), out_shape=...  115 us
    pallas_call x1, Pallas kernels, body(): pl.pallas_call(functools.partial(finish_kernel, n_rcv), out_shape=jax.Sha...  3.72 us

profile of v3, /device:TPU:0, one launch (start us, length us, event | category | flops | bytes accessed | tf_op | source)
XLA Modules:
  0.0 118.7 jit_solution(16318602609850652750)
XLA Ops:
  0.0 114.9 %ring_products.1 = (f32[16,2,256,256]{3,2,1,0:T(8,128)S(1)}, bf16[2,22,128,256]{3,2,1,0:T(8,128)(2,1)S(1)}, f32[2,128,128]{2,1,0:T(8,128)S(1)}, s32[2,256]{1,0:T(2,128)S(4)}) custom-call(s32[1024]{0:T(1024)} %stations_in.1, s32[2,256]{1,0:T(2,128)} %bitcast.5, f32[2,128,2816]{2,1,0:T(8,128)} %panel.1, f32[1024,2,128]{2,1,0:T(2,128)} %bitcast.4, ...), custom_call_target="tpu_custom_call" | custom-call | tf_op jit(solution)/shard_map/ring_products/pallas_call | solution.py:359
  114.9 3.7 %last_products.1 = f32[16,2,256,256]{3,2,1,0:T(8,128)} custom-call(s32[2,256]{1,0:T(2,128)S(4)} %get-tuple-element.9.tiles, f32[2,128,128]{2,1,0:T(8,128)S(1)} %get-tuple-element.10.weight, bf16[2,22,128,256]{3,2,1,0:T(8,128)(2,1)S(1)} %get-tuple-element.11.last, f32[16,2,256,256]{3,2,1,0:T(8,128)S(1)} %get-tuple-element.12.acc), custom_call_target="tpu_custom_call" | custom-call | tf_op jit(solution)/shard_map/last_products/pallas_call | solution.py:390

commit v4 on v3

--- a/solution.py
+++ b/solution.py
@@ -64,7 +64,7 @@
 
 
 def first_pieces(held):
-    small = min(2, held - 1)
+    small = min(4, held - 1)
     return [(0, small), (small, held - small)]
 
 
@@ -97,15 +97,13 @@
         at = (part, slice(None), pl.ds(cuts[c][0] * side, cuts[c][1] * side))
         return pltpu.make_async_copy(panel.at[at], stage.at[at], load_sem.at[part, c])
 
-    for part in (0, 1):
-        load(part, 0).start()
     barrier = pltpu.get_barrier_semaphore()
     for peer in (left, right):
         pl.semaphore_signal(barrier, inc=1, device_id={"src": peer}, device_id_type=MESH)
     for off in range(1, n_rcv):
         pl.semaphore_signal(barrier, inc=1, device_id={"rcv": (rcv + off) % n_rcv}, device_id_type=MESH)
 
-    for c in range(1, len(cuts)):
+    for c in range(len(cuts)):
         for part in (0, 1):
             load(part, c).start()
     named = pltpu.make_async_copy(stations_in, stations, local_sem.at[2])

time: 119 us -> 119 us (level)
  no operation moved by 1% of the time
where the time goes in v4:
time: 119 us
  Pallas kernels  119 us (100%)
    pallas_call x1, Pallas kernels, body(): pl.pallas_call(functools.partial(gather_kernel, n_src, n_rcv), out_shape=...  115 us
    pallas_call x1, Pallas kernels, body(): pl.pallas_call(functools.partial(finish_kernel, n_rcv), out_shape=jax.Sha...  3.72 us

profile of v4, /device:TPU:0, one launch (start us, length us, event | category | flops | bytes accessed | tf_op | source)
XLA Modules:
  0.0 118.7 jit_solution(850526268342578090)
XLA Ops:
  0.0 114.9 %ring_products.1 = (f32[16,2,256,256]{3,2,1,0:T(8,128)S(1)}, bf16[2,22,128,256]{3,2,1,0:T(8,128)(2,1)S(1)}, f32[2,128,128]{2,1,0:T(8,128)S(1)}, s32[2,256]{1,0:T(2,128)S(4)}) custom-call(s32[1024]{0:T(1024)} %stations_in.1, s32[2,256]{1,0:T(2,128)} %bitcast.5, f32[2,128,2816]{2,1,0:T(8,128)} %panel.1, f32[1024,2,128]{2,1,0:T(2,128)} %bitcast.4, ...), custom_call_target="tpu_custom_call" | custom-call | tf_op jit(solution)/shard_map/ring_products/pallas_call | solution.py:357
  115.0 3.7 %last_products.1 = f32[16,2,256,256]{3,2,1,0:T(8,128)} custom-call(s32[2,256]{1,0:T(2,128)S(4)} %get-tuple-element.9.tiles, f32[2,128,128]{2,1,0:T(8,128)S(1)} %get-tuple-element.10.weight, bf16[2,22,128,256]{3,2,1,0:T(8,128)(2,1)S(1)} %get-tuple-element.11.last, f32[16,2,256,256]{3,2,1,0:T(8,128)S(1)} %get-tuple-element.12.acc), custom_call_target="tpu_custom_call" | custom-call | tf_op jit(solution)/shard_map/last_products/pallas_call | solution.py:388

commit v5 on v3

--- a/solution.py
+++ b/solution.py
@@ -71,7 +71,7 @@
 def last_pieces(n_rcv, held):
     if n_rcv != 2 or held < 6:
         return [[(r * held, held - 1), (r * held + held - 1, 1)] for r in range(n_rcv)]
-    return [[(0, held - 3), (held - 3, 2)], [(held + 1, held - 1), (held - 1, 2)]]
+    return [[(0, held - 5), (held - 5, 3)], [(held + 2, held - 2), (held - 2, 4)]]
 
 
 def gather_kernel(n_src, n_rcv, stations_in, tiles_in, panel, lines, recorded, acc, last, weight_out, tiles, *scratch):

time: 119 us -> 119 us (level)
  no operation moved by 1% of the time
where the time goes in v5:
time: 119 us
  Pallas kernels  119 us (100%)
    pallas_call x1, Pallas kernels, body(): pl.pallas_call(functools.partial(gather_kernel, n_src, n_rcv), out_shape=...  115 us
    pallas_call x1, Pallas kernels, body(): pl.pallas_call(functools.partial(finish_kernel, n_rcv), out_shape=jax.Sha...  3.72 us

profile of v5, /device:TPU:0, one launch (start us, length us, event | category | flops | bytes accessed | tf_op | source)
XLA Modules:
  0.0 119.0 jit_solution(9313191046883749647)
XLA Ops:
  0.0 115.3 %ring_products.1 = (f32[16,2,256,256]{3,2,1,0:T(8,128)S(1)}, bf16[2,22,128,256]{3,2,1,0:T(8,128)(2,1)S(1)}, f32[2,128,128]{2,1,0:T(8,128)S(1)}, s32[2,256]{1,0:T(2,128)S(4)}) custom-call(s32[1024]{0:T(1024)} %stations_in.1, s32[2,256]{1,0:T(2,128)} %bitcast.5, f32[2,128,2816]{2,1,0:T(8,128)} %panel.1, f32[1024,2,128]{2,1,0:T(2,128)} %bitcast.4, ...), custom_call_target="tpu_custom_call" | custom-call | tf_op jit(solution)/shard_map/ring_products/pallas_call | solution.py:359
  115.3 3.7 %last_products.1 = f32[16,2,256,256]{3,2,1,0:T(8,128)} custom-call(s32[2,256]{1,0:T(2,128)S(4)} %get-tuple-element.9.tiles, f32[2,128,128]{2,1,0:T(8,128)S(1)} %get-tuple-element.10.weight, bf16[2,22,128,256]{3,2,1,0:T(8,128)(2,1)S(1)} %get-tuple-element.11.last, f32[16,2,256,256]{3,2,1,0:T(8,128)S(1)} %get-tuple-element.12.acc), custom_call_target="tpu_custom_call" | custom-call | tf_op jit(solution)/shard_map/last_products/pallas_call | solution.py:390
